TPU v7x, 32 devices: a whole 2x2x4 slice. The times are simulated.
32 devices in a mesh: ep: 4 (over x, core), fsdp: 8 (over z, y).
Axes of the slice: x: 2, y: 2, z: 4, core: 2. Of those that a mesh axis runs over, the one named last changes fastest.
Arguments:
- train_gate: float32 [128, 2048, 768], P('ep', 'fsdp'), may hold values from -0.1875 to 0.1875
- other_gate: bfloat16 [128, 2048, 768], P('ep', 'fsdp'), may hold values from -0.0625 to 0.0625
- train_up: float32 [128, 2048, 768], P('ep', 'fsdp'), may hold values from -0.1875 to 0.1875
- other_up: bfloat16 [128, 2048, 768], P('ep', 'fsdp'), may hold values from -0.0625 to 0.0625
- router_weight: float32 [2048, 128], P('fsdp', 'ep'), may hold values from -0.125 to 0.125
- router_gain: float32 [2048], P('fsdp'), may hold values from 0.25 to 1.75
Outputs:
- ready_gate: bfloat16 [128, 2048, 768], P('ep', None, 'fsdp')
- ready_up: bfloat16 [128, 2048, 768], P('ep', None, 'fsdp')
- scale_gate: float32 [128, 768], P('ep', 'fsdp')
- scale_up: float32 [128, 768], P('ep', 'fsdp')
- serve_router: bfloat16 [2048, 128], replicated
All inputs are finite; a program needn't handle non-finite values. Where the computation divides by a largest or mean magnitude, that divisor is 1e-20 or more.
Results may differ from a plain program's by a relative error of at most 0.001.
Values may be sent and summed in bfloat16 or wider, within the bound.
A program may use at most 256 MiB of HBM per device.

v0:
```python
import jax
import jax.numpy as jnp
from jax import lax
from jax.sharding import PartitionSpec as P

D_MODEL = 2048


def per_device(train_gate, other_gate, train_up, other_up, router_weight, router_gain):
    latest_gate = train_gate + other_gate.astype(jnp.float32)
    latest_up = train_up + other_up.astype(jnp.float32)
    total_gate, total_up = lax.psum(
        (jnp.sum(jnp.abs(latest_gate), axis=1), jnp.sum(jnp.abs(latest_up), axis=1)), "fsdp"
    )
    scale_gate = total_gate / D_MODEL
    scale_up = total_up / D_MODEL
    narrow_gate, narrow_up = (
        (latest_gate / jnp.expand_dims(scale_gate, 1)).astype(jnp.bfloat16),
        (latest_up / jnp.expand_dims(scale_up, 1)).astype(jnp.bfloat16),
    )
    ready_gate, ready_up = (
        lax.all_to_all(narrow_gate, "fsdp", split_axis=2, concat_axis=1, tiled=True),
        lax.all_to_all(narrow_up, "fsdp", split_axis=2, concat_axis=1, tiled=True),
    )
    scale_gate = lax.dynamic_slice_in_dim(
        scale_gate, lax.axis_index("fsdp") * ready_gate.shape[2], ready_gate.shape[2], axis=1
    )
    scale_up = lax.dynamic_slice_in_dim(
        scale_up, lax.axis_index("fsdp") * ready_up.shape[2], ready_up.shape[2], axis=1
    )
    part_router = (router_weight * router_gain[:, None]).astype(jnp.bfloat16)
    row_router = lax.all_gather(part_router, "fsdp", axis=0, tiled=True)
    serve_router = lax.all_gather(row_router, "ep", axis=1, tiled=True)
    return (ready_gate, ready_up, scale_gate, scale_up, serve_router)


def solution(mesh):
    in_specs = (
        P("ep", "fsdp", None),
        P("ep", "fsdp", None),
        P("ep", "fsdp", None),
        P("ep", "fsdp", None),
        P("fsdp", "ep"),
        P("fsdp"),
    )
    out_specs = (
        P("ep", None, "fsdp"),
        P("ep", None, "fsdp"),
        P("ep", "fsdp"),
        P("ep", "fsdp"),
        P(),
    )
    return jax.shard_map(
        per_device, mesh=mesh, in_specs=in_specs, out_specs=out_specs, check_vma=False
    )
```

profile of v0, /device:TPU:0, one launch (start us, length us, event | category | flops | bytes accessed | tf_op | source)
XLA Modules:
  0.0 870.3 jit_solution(15203372725488731711)
XLA Ops:
  7.2 0.0 all-reduce.3.cloned.1.call-start
  7.2 25.1 %copy.38 = f32[32,256,768]{1,0,2:T(8,128)} copy(f32[32,256,768]{2,1,0:T(8,128)} %param.6) | data formatting | bytes 50331648 | tf_op args[0]
  32.3 25.1 %copy.42 = f32[32,256,768]{1,0,2:T(8,128)} copy(f32[32,256,768]{2,1,0:T(8,128)} %param.8) | data formatting | bytes 50331648 | tf_op args[2]
  57.4 16.9 %copy.37 = bf16[32,256,768]{1,0,2:T(8,128)(2,1)} copy(bf16[32,256,768]{2,1,0:T(8,128)(2,1)} %param.7) | data formatting | bytes 25165824 | tf_op args[1]
  74.2 16.9 %copy.41 = bf16[32,256,768]{1,0,2:T(8,128)(2,1)} copy(bf16[32,256,768]{2,1,0:T(8,128)(2,1)} %param.9) | data formatting | bytes 25165824 | tf_op args[3]
  91.1 25.2 %abs_reduce_fusion = (f32[32,768]{0,1:T(8,128)}, f32[32,768]{0,1:T(8,128)}) fusion(f32[32,256,768]{1,0,2:T(8,128)} %copy.42, bf16[32,256,768]{1,0,2:T(8,128)(2,1)} %copy.41, f32[32,256,768]{1,0,2:T(8,128)} %copy.38, bf16[32,256,768]{1,0,2:T(8,128)(2,1)} %copy.37), kind=kLoop, calls=%fused_computation.1 | loop fusion | flops 50282496 | bytes 75694080 | tf_op jit(solution)/shard_map/reduce_sum | solution.py:13
  116.3 0.0 all-reduce.3.cloned.1.call-update
  116.3 78.0 %all-reduce.3.cloned.1.call-done = (f32[32,768]{0,1:T(8,128)}, f32[32,768]{0,1:T(8,128)}) async-done(((f32[32,768]{0,1:T(8,128)}, f32[32,768]{0,1:T(8,128)}), (f32[32,768]{0,1:T(8,128)}, f32[32,768]{0,1:T(8,128)})) %all-reduce.3.cloned.1.call-update) | async-done | bytes 196624 | tf_op jit(solution)/shard_map/psum | solution.py:12
  194.4 1.0 broadcast_multiply_fusion
  195.4 16.9 %divide_convert_fusion = bf16[32,256,768]{1,0,2:T(8,128)(2,1)} fusion(f32[32,256,768]{1,0,2:T(8,128)} %copy.42, bf16[32,256,768]{1,0,2:T(8,128)(2,1)} %copy.41, f32[32,768]{0,1:T(8,128)S(1)} %broadcast_multiply_fusion), kind=kLoop, calls=%fused_computation | loop fusion | flops 25165824 | bytes 50429952 | tf_op jit(solution)/shard_map/convert_element_type | solution.py:19
  212.3 0.0 copy-start
  212.3 5.5 all-to-all-start.1
  217.9 0.0 copy-done
  217.9 17.0 %divide_convert_fusion.1 = bf16[32,256,768]{1,0,2:T(8,128)(2,1)} fusion(f32[32,256,768]{1,0,2:T(8,128)} %copy.38, bf16[32,256,768]{1,0,2:T(8,128)(2,1)} %copy.37, f32[32,768]{0,1:T(8,128)S(1)} %broadcast_multiply_fusion.1), kind=kLoop, calls=%fused_computation.3 | loop fusion | flops 25165824 | bytes 50429952 | tf_op jit(solution)/shard_map/convert_element_type | solution.py:18
  234.9 0.0 copy-start.1
  234.9 0.0 copy-start.2
  234.9 255.0 %all-to-all-done.1 = bf16[32,256,768]{1,0,2:T(8,128)(2,1)} async-done(((bf16[32,256,768]{1,0,2:T(8,128)(2,1)}), bf16[32,256,768]{1,0,2:T(8,128)(2,1)}, u32[]{:S(2)}, u32[]{:S(2)}) %all-to-all-start.1) | async-done | bytes 12582944 | tf_op jit(solution)/shard_map/all_to_all | solution.py:23
  489.9 5.4 all-to-all-start
  495.3 0.0 copy-done.1
  495.3 0.0 copy-done.2
  495.3 291.6 %all_gather.6 = bf16[2048,32]{0,1:T(8,128)(2,1)S(1)} all-gather(bf16[256,32]{0,1:T(8,128)(2,1)S(1)} %multiply_convert_fusion), channel_id=1, replica_groups=mesh['ep'=4,'fsdp'=8] {'fsdp'}, dimensions={0}, use_global_device_ids=true | all-gather | bytes 147456 | tf_op jit(solution)/shard_map/all_gather | solution.py:32
  786.9 7.1 all_gather.7
  794.0 1.0 copy.47
  795.0 0.7 copy.45
  795.7 0.7 copy.46
  796.3 14.1 %copy.44 = bf16[32,8,256,96]{2,1,3,0:T(8,128)(2,1)} copy(bf16[32,8,256,96]{2,0,3,1:T(8,128)(2,1)} %bitcast.5) | data formatting | bytes 25165824 | tf_op jit(solution)/shard_map/all_to_all | solution.py:23
  810.4 19.5 %all_to_all.33 = bf16[32,2048,96]{1,2,0:T(8,128)(2,1)} reshape(bf16[32,8,256,96]{2,1,3,0:T(8,128)(2,1)} %copy.44) | data formatting | bytes 25165824 | tf_op jit(solution)/shard_map/all_to_all | solution.py:23
  829.9 0.0 all-to-all-done
  829.9 14.1 %copy.40 = bf16[32,8,256,96]{2,1,3,0:T(8,128)(2,1)} copy(bf16[32,8,256,96]{2,0,3,1:T(8,128)(2,1)} %bitcast.2) | data formatting | bytes 25165824 | tf_op jit(solution)/shard_map/all_to_all | solution.py:22
  844.0 19.5 %all_to_all.29 = bf16[32,2048,96]{1,2,0:T(8,128)(2,1)} reshape(bf16[32,8,256,96]{2,1,3,0:T(8,128)(2,1)} %copy.40) | data formatting | bytes 25165824 | tf_op jit(solution)/shard_map/all_to_all | solution.py:22
  (4 shorter events, 0.0 us)
Async XLA Ops:
  7.2 187.2 %all-reduce.3.cloned.1.call-start = ((), (), s32[]{:S(2)}) async-start(), calls=%async_computation.2 | async-start | bytes 1572864 | tf_op jit(solution)/shard_map/psum | solution.py:12
  212.3 5.6 copy-start
  212.3 277.6 %all-to-all-start.1 = ((bf16[32,256,768]{1,0,2:T(8,128)(2,1)}), bf16[32,256,768]{1,0,2:T(8,128)(2,1)}, u32[]{:S(2)}, u32[]{:S(2)}) async-start(bf16[32,256,768]{1,0,2:T(8,128)(2,1)} %divide_convert_fusion), calls=%async_computation.1 | async-start | bytes 25165824 | tf_op jit(solution)/shard_map/all_to_all | solution.py:23
  234.9 260.4 %copy-start.1 = (f32[256,32]{0,1:T(8,128)S(1)}, f32[256,32]{0,1:T(8,128)}, u32[]{:S(2)}) copy-start(f32[256,32]{0,1:T(8,128)} %param.10) | copy-start | bytes 98308
  234.9 260.4 %copy-start.2 = (f32[256]{0:T(256)S(1)}, f32[256]{0:T(256)}, u32[]{:S(2)}) copy-start(f32[256]{0:T(256)} %param.11) | copy-start | bytes 3076
  489.9 340.0 %all-to-all-start = ((bf16[32,256,768]{1,0,2:T(8,128)(2,1)}), bf16[32,256,768]{1,0,2:T(8,128)(2,1)}, u32[]{:S(2)}, u32[]{:S(2)}) async-start(bf16[32,256,768]{1,0,2:T(8,128)(2,1)} %divide_convert_fusion.1), calls=%async_computation | async-start | bytes 25165824 | tf_op jit(solution)/shard_map/all_to_all | solution.py:22
Sparse Core Ops, SparseCore 0:
  116.4 77.8 all-reduce.2
where the time goes:
time: 873 us; the launch traced here: 870 us
  waiting for transfers between devices  333 us (38%)
  blocking collectives  299 us (34%)
  local copies, waits for them, and re-layouts  153 us (18%)
  other arithmetic  60.2 us (7%)
  between operations  14.1 us (2%)
  starting transfers between devices  10.9 us (1%)
    all_gather x1, blocking collectives, per_device(): row_router = lax.all_gather(part_router, 'fsdp', axis=0, tiled=True)  292 us
    all_to_all x1, waiting for transfers between devices, per_device(): lax.all_to_all(narrow_up, 'fsdp', split_axis=2, concat_axis=1, tiled=True)  255 us
    unnamed x13, local copies, waits for them, and re-layouts  86.2 us
    psum x1, waiting for transfers between devices, per_device(): lax.psum((jnp.sum(jnp.abs(latest_gate), axis=1), jnp.sum(jnp.abs(latest_u...  78 us
    all_to_all x2, local copies, waits for them, and re-layouts, per_device(): lax.all_to_all(narrow_gate, 'fsdp', split_axis=2, concat_axis=1, tiled=True)  33.6 us
    all_to_all x2, local copies, waits for them, and re-layouts, per_device(): lax.all_to_all(narrow_up, 'fsdp', split_axis=2, concat_axis=1, tiled=True)  33.6 us
    reduce_sum x1, other arithmetic, per_device(): jnp.sum(jnp.abs(latest_up), axis=1)  25.2 us
  transfers between devices with their start and end apart: 3, of which 2 were waited for; matrix products, arithmetic and copies ran while one was open for 4% of the time, Pallas kernels for 0%

commit v1 on v0

v1 whole, which is shorter than its diff:
```python
import functools

import jax
import jax.numpy as jnp
from jax import lax
from jax.experimental import pallas as pl
from jax.experimental.pallas import tpu as pltpu
from jax.sharding import PartitionSpec as P

MESH = pl.DeviceIdType.MESH
SLOTS = 3


def plain_device(train_gate, other_gate, train_up, other_up, router_weight, router_gain):
    latest_gate = train_gate + other_gate.astype(jnp.float32)
    latest_up = train_up + other_up.astype(jnp.float32)
    depth = train_gate.shape[1] * lax.axis_size("fsdp")
    total_gate, total_up = lax.psum(
        (jnp.sum(jnp.abs(latest_gate), axis=1), jnp.sum(jnp.abs(latest_up), axis=1)), "fsdp"
    )
    scale_gate = total_gate / depth
    scale_up = total_up / depth
    narrow_gate = (latest_gate / jnp.expand_dims(scale_gate, 1)).astype(jnp.bfloat16)
    narrow_up = (latest_up / jnp.expand_dims(scale_up, 1)).astype(jnp.bfloat16)
    ready_gate = lax.all_to_all(narrow_gate, "fsdp", split_axis=2, concat_axis=1, tiled=True)
    ready_up = lax.all_to_all(narrow_up, "fsdp", split_axis=2, concat_axis=1, tiled=True)
    width = ready_gate.shape[2]
    start = lax.axis_index("fsdp") * width
    scale_gate = lax.dynamic_slice_in_dim(scale_gate, start, width, axis=1)
    scale_up = lax.dynamic_slice_in_dim(scale_up, start, width, axis=1)
    part_router = (router_weight * router_gain[:, None]).astype(jnp.bfloat16)
    row_router = lax.all_gather(part_router, "fsdp", axis=0, tiled=True)
    serve_router = lax.all_gather(row_router, "ep", axis=1, tiled=True)
    return (ready_gate, ready_up, scale_gate, scale_up, serve_router)


def far_first(n):
    return sorted(range(1, n), key=lambda d: (abs(d - n // 2), d))


def kernel(n, p, tg, og, tu, ou, rw, rgain, ready_gate, ready_up, scale_gate, scale_up, router,
           wide, narrow, send, part_a, land_a, tot_a, part_b, land_b, tot_b, rows_r, all_r,
           in_sem, own_sem, send_sem, recv_sem, small_send, small_recv, r_send, r_recv):
    experts, depth, width = tg.shape
    piece = width // n
    me = lax.axis_index("fsdp")
    group = lax.axis_index("ep")
    first = n // 2
    trains, others = (tg, tu), (og, ou)
    readys, scales = (ready_gate, ready_up), (scale_gate, scale_up)
    peers = [(me + d) % n for d in far_first(n)]
    twins = [(group + d) % p for d in range(1, p)]

    barrier = pltpu.get_barrier_semaphore()
    for peer in peers:
        pl.semaphore_signal(barrier, inc=1, device_id={"fsdp": peer}, device_id_type=MESH)
    for twin in twins:
        pl.semaphore_signal(barrier, inc=1, device_id={"ep": twin}, device_id_type=MESH)

    def loads(e, slot):
        return [
            pltpu.make_async_copy(src.at[e], dst.at[m, slot], in_sem.at[k, m, slot])
            for m in range(2)
            for k, (src, dst) in enumerate(((trains[m], wide), (others[m], narrow)))
        ]

    def over(low, high, body):
        for e in range(low, min(low + SLOTS - 1, high)):
            for copy in loads(e, (e - low) % SLOTS):
                copy.start()

        def step(i, _):
            e = low + i
            slot = lax.rem(i, SLOTS)

            @pl.when(e + SLOTS - 1 < high)
            def _():
                for copy in loads(e + SLOTS - 1, lax.rem(i + SLOTS - 1, SLOTS)):
                    copy.start()

            for copy in loads(e, slot):
                copy.wait()
            for m in range(2):
                body(e, m, slot)
            return 0

        lax.fori_loop(0, high - low, step, 0)

    def sums(base, part, share):
        def body(e, m, slot):
            at = (e - base) * 2 + m
            latest = wide[m, slot] + narrow[m, slot].astype(jnp.float32)
            row = jnp.sum(jnp.abs(latest), axis=0, keepdims=True)
            part[at // share, pl.ds(at % share, 1), :] = row

        return body

    def ready(base, tot, share):
        def body(e, m, slot):
            at = (e - base) * 2 + m
            scale = tot[at // share, pl.ds(at % share, 1), :] / (n * depth)
            scales[m][pl.ds(e, 1), :] = scale
            inverse = 1.0 / scale
            step = 128
            for c in range(0, width, step):
                latest = wide[m, slot, :, c:c + step] + narrow[m, slot, :, c:c + step].astype(jnp.float32)
                value = latest * inverse[:, c:c + step]
                send[m, e, c:c + step, :] = value.T.astype(jnp.bfloat16)
            place = readys[m].at[e, :, pl.ds(pl.multiple_of(me * depth, 128), depth)]
            for peer in peers:
                pltpu.make_async_remote_copy(
                    src_ref=send.at[m, e, pl.ds(pl.multiple_of(peer * piece, 16), piece), :],
                    dst_ref=place,
                    send_sem=send_sem.at[m],
                    recv_sem=recv_sem.at[m],
                    device_id={"fsdp": peer},
                    device_id_type=MESH,
                ).start()
            pltpu.make_async_copy(
                send.at[m, e, pl.ds(pl.multiple_of(me * piece, 16), piece), :], place, own_sem.at[m]
            ).start()

        return body

    def push(src, dst, at, axis, targets, s, r):
        for target, block in zip(targets, src):
            pltpu.make_async_remote_copy(
                src_ref=block, dst_ref=dst.at[at], send_sem=s, recv_sem=r,
                device_id={axis: target}, device_id_type=MESH,
            ).start()

    def drain(ref, sem):
        pltpu.make_async_copy(ref, ref, sem).wait()

    def scatter(part, land, k):
        push([part.at[peer] for peer in peers], land, me, "fsdp", peers, small_send.at[k], small_recv.at[k])
        land[me] = part[me]

    def gather(land, tot, k):
        drain(land.at[pl.ds(0, n - 1)], small_recv.at[k])
        tot[me] = jnp.sum(land[...], axis=0)
        push([tot.at[me]] * (n - 1), tot, me, "fsdp", peers, small_send.at[k + 1], small_recv.at[k + 1])

    def gathered(tot, k):
        drain(tot.at[pl.ds(0, n - 1)], small_recv.at[k + 1])

    share_b = part_b.shape[1]
    over(0, first, sums(0, part_a, 1))
    rows_r[me] = (rw[...] * rgain[...]).astype(jnp.bfloat16)
    pl.semaphore_wait(barrier, n - 1 + p - 1)
    scatter(part_a, land_a, 0)
    gather(land_a, tot_a, 0)
    gathered(tot_a, 0)
    cut = max(first // 2, 1)
    over(0, cut, ready(0, tot_a, 1))
    over(first, experts, sums(first, part_b, share_b))
    scatter(part_b, land_b, 2)
    push([rows_r.at[me]] * (n - 1), rows_r, me, "fsdp", peers, r_send.at[0], r_recv.at[0])
    middle = (cut + first) // 2
    over(cut, middle, ready(0, tot_a, 1))
    gather(land_b, tot_b, 2)
    over(middle, first, ready(0, tot_a, 1))
    gathered(tot_b, 2)
    later = first + (experts - first) // 4
    over(first, later, ready(first, tot_b, share_b))
    drain(rows_r.at[pl.ds(0, n - 1)], r_recv.at[0])
    push([rows_r] * (p - 1), all_r, group, "ep", twins, r_send.at[1], r_recv.at[1])
    all_r[group] = rows_r[...]
    over(later, experts, ready(first, tot_b, share_b))
    if p > 1:
        drain(all_r.at[pl.ds(0, p - 1)], r_recv.at[1])
    for f in range(n):
        block = all_r[:, f].astype(jnp.float32)
        block = block.reshape(block.shape[0] * block.shape[1], depth)
        router[f * depth:(f + 1) * depth, :] = block.T.astype(jnp.bfloat16)
    for k, (part, tot) in enumerate(((part_a, tot_a), (part_b, tot_b))):
        drain(part.at[pl.ds(0, n - 1)], small_send.at[2 * k])
        drain(tot.at[pl.ds(0, n - 1)], small_send.at[2 * k + 1])
    drain(rows_r.at[pl.ds(0, n - 1)], r_send.at[0])
    if p > 1:
        drain(all_r.at[pl.ds(0, p - 1)], r_send.at[1])
    for m in range(2):
        drain(send.at[m, :, pl.ds(0, piece), :], own_sem.at[m])
        drain(send.at[m, :, pl.ds(0, width - piece), :], send_sem.at[m])
        drain(readys[m].at[:, :, pl.ds(0, (n - 1) * depth)], recv_sem.at[m])


def sending_device(n, p, train_gate, other_gate, train_up, other_up, router_weight, router_gain):
    experts, depth, width = train_gate.shape
    piece = width // n
    columns = router_weight.shape[1]
    share = (2 * experts - n) // n
    f32, bf16 = jnp.float32, jnp.bfloat16
    anywhere = pl.BlockSpec(memory_space=pl.ANY)
    vmem = pl.BlockSpec(memory_space=pltpu.VMEM)
    ready = jax.ShapeDtypeStruct((experts, piece, n * depth), bf16)
    scale = jax.ShapeDtypeStruct((experts, width), f32)
    stats = [pltpu.VMEM((n, 1, width), f32)] * 3 + [pltpu.VMEM((n, share, width), f32)] * 3
    dma = pltpu.SemaphoreType.DMA
    ready_gate, ready_up, scale_gate, scale_up, router = pl.pallas_call(
        functools.partial(kernel, n, p),
        out_shape=(ready, ready, scale, scale, jax.ShapeDtypeStruct((n * depth, p * columns), bf16)),
        in_specs=[anywhere] * 4 + [vmem] * 2,
        out_specs=(anywhere, anywhere, vmem, vmem, vmem),
        scratch_shapes=[
            pltpu.VMEM((2, SLOTS, depth, width), f32),
            pltpu.VMEM((2, SLOTS, depth, width), bf16),
            pltpu.VMEM((2, experts, width, depth), bf16),
            *stats,
            pltpu.VMEM((n, columns, depth), bf16),
            pltpu.VMEM((p, n, columns, depth), bf16),
            dma((2, 2, SLOTS)), dma((2,)), dma((2,)), dma((2,)), dma((4,)), dma((4,)), dma((2,)), dma((2,)),
        ],
        compiler_params=pltpu.CompilerParams(
            collective_id=0, has_side_effects=True, vmem_limit_bytes=60 * 2**20
        ),
        name="send_ready",
    )(train_gate, other_gate, train_up, other_up, router_weight.T, router_gain[None, :])
    start = lax.axis_index("fsdp") * piece
    return (
        jnp.swapaxes(ready_gate, 1, 2),
        jnp.swapaxes(ready_up, 1, 2),
        lax.dynamic_slice_in_dim(scale_gate, start, piece, axis=1),
        lax.dynamic_slice_in_dim(scale_up, start, piece, axis=1),
        router,
    )


def solution(mesh):
    n, p = mesh.shape["fsdp"], mesh.shape["ep"]

    def per_device(*args):
        experts, depth, width = args[0].shape
        fits = (
            depth % 128 == 0 and width % (16 * n) == 0 and width % 128 == 0 and n % 2 == 0
            and 2 * experts % n == 0 and 2 * experts > n and args[4].shape[1] % 16 == 0
            and 2 * experts * depth * width * 2 <= 2**25
        )
        return sending_device(n, p, *args) if fits else plain_device(*args)

    matrix = P("ep", "fsdp", None)
    in_specs = (matrix, matrix, matrix, matrix, P("fsdp", "ep"), P("fsdp"))
    out_specs = (P("ep", None, "fsdp"), P("ep", None, "fsdp"), P("ep", "fsdp"), P("ep", "fsdp"), P())
    return jax.shard_map(
        per_device, mesh=mesh, in_specs=in_specs, out_specs=out_specs, check_vma=False
    )
```

time: 873 us -> 591 us (0.68)
  Pallas kernels: 0 us -> 570 us
  waiting for transfers between devices: 333 us -> 0 us
  blocking collectives: 299 us -> 0 us
  local copies, waits for them, and re-layouts: 153 us -> 20 us
  other arithmetic: 60.2 us -> 0 us
  between operations: 14.1 us -> 0.65 us
  starting transfers between devices: 10.9 us -> 0 us
    pallas_call x0 -> x1, Pallas kernels: none -> 570 us  [sending_device(): pl.pallas_call(functools.partial(kernel, n, p), out_shape=(ready, ready,...]
    all_gather x2 -> x0, blocking collectives: 299 us -> none  [the longest x1 292 us: per_device(): row_router = lax.all_gather(part_router, 'fsdp', axis=0, tiled=True)]
    all_to_all x2 -> x0, waiting for transfers between devices: 255 us -> none  [the longest x1 255 us: per_device(): lax.all_to_all(narrow_up, 'fsdp', split_axis=2, concat_axis=1, tiled=True)]
    psum x1 -> x0, waiting for transfers between devices: 78 us -> none  [per_device(): lax.psum((jnp.sum(jnp.abs(latest_gate), axis=1), jnp.sum(jnp.abs(latest_u...]
    unnamed x13 -> x7, local copies, waits for them, and re-layouts: 86.2 us -> 18.5 us
    all_to_all x4 -> x0, local copies, waits for them, and re-layouts: 67.1 us -> none  [the longest x2 33.6 us: per_device(): lax.all_to_all(narrow_gate, 'fsdp', split_axis=2, concat_axis=1, tiled=True)]
    convert_element_type x3 -> x0, other arithmetic: 33.9 us -> none  [the longest x1 17 us: per_device(): (latest_gate / jnp.expand_dims(scale_gate, 1)).astype(jnp.bfloat16)]
    reduce_sum x1 -> x0, other arithmetic: 25.2 us -> none  [per_device(): jnp.sum(jnp.abs(latest_up), axis=1)]
  transfers between devices with their start and end apart: 3 -> 0, of which waited for: 2 -> 0; matrix products, arithmetic and copies ran while one was open for 4% -> 0% of each run, Pallas kernels for 0% -> 0%
where the time goes in v1:
time: 591 us; the launch traced here: 590 us
  Pallas kernels  570 us (96%)
  local copies, waits for them, and re-layouts  20 us (3%)
    pallas_call x1, Pallas kernels, sending_device(): pl.pallas_call(functools.partial(kernel, n, p), out_shape=(ready, ready,...  570 us
    unnamed x7, local copies, waits for them, and re-layouts  18.5 us

profile of v1, /device:TPU:0, one launch (start us, length us, event | category | flops | bytes accessed | tf_op | source)
XLA Modules:
  0.0 590.4 jit_solution(3386432509079304458)
XLA Ops:
  0.6 569.8 %send_ready.1 = (bf16[32,96,2048]{2,1,0:T(8,128)(2,1)}, bf16[32,96,2048]{2,1,0:T(8,128)(2,1)}, f32[32,768]{1,0:T(8,128)}, f32[32,768]{1,0:T(8,128)}, bf16[2048,128]{1,0:T(8,128)(2,1)}) custom-call(f32[32,256,768]{2,1,0:T(8,128)} %tg.1, bf16[32,256,768]{2,1,0:T(8,128)(2,1)} %og.1, f32[32,256,768]{2,1,0:T(8,128)} %tu.1, bf16[32,256,768]{2,1,0:T(8,128)(2,1)} %ou.1, ...), custom_call_target="tpu_custom_call" | custom-call | tf_op jit(solution)/shard_map/send_ready/pallas_call | solution.py:200
  570.5 1.5 constant_dynamic-slice_fusion
  572.0 0.0 copy-start
  572.0 11.4 %copy.14 = bf16[32,2048,96]{1,2,0:T(8,128)(2,1)} copy(bf16[32,2048,96]{1,2,0:T(8,128)(2,1)} %bitcast.5) | data formatting | bytes 25165824
  583.3 1.5 copy-done
  584.9 0.0 copy-start.1
  584.9 4.8 copy.15
  589.6 0.0 copy-done.1
  589.6 0.8 copy.16
Async XLA Ops:
  572.0 12.9 %copy-start = (bf16[32,96,2048]{2,1,0:T(8,128)(2,1)S(1)}, bf16[32,96,2048]{2,1,0:T(8,128)(2,1)}, u32[]{:S(2)}) copy-start(bf16[32,96,2048]{2,1,0:T(8,128)(2,1)} %get-tuple-element.11) | copy-start | bytes 37748740
  584.9 4.8 copy-start.1
